TPU v7x, 32 devices: a whole 2x2x4 slice. The times are simulated.
32 devices in a mesh: fsdp: 4 (over x, core), ctx: 8 (over z, y).
Axes of the slice: x: 2, y: 2, z: 4, core: 2. Of those that a mesh axis runs over, the one named last changes fastest.
Arguments:
- inputs: bfloat16 [4096, 1536], P(('fsdp', 'ctx')), may hold values from -6 to 6
- positions: int32 [4096], P(('fsdp', 'ctx')), may hold values from 0 to 1023, as said below
- cotangent: bfloat16 [4096, 1536], P(('fsdp', 'ctx')), may hold values from -6 to 6
- attention_gain: bfloat16 [1536], replicated, may hold values from 0.5 to 1.5
- query_weight: bfloat16 [1536, 1536], P('fsdp'), may hold values from -0.15625 to 0.15625
- key_weight: bfloat16 [768, 1536], P('fsdp'), may hold values from -0.15625 to 0.15625
- value_weight: bfloat16 [768, 1536], P('fsdp'), may hold values from -0.15625 to 0.15625
- output_weight: bfloat16 [1536, 1536], P('fsdp'), may hold values from -3 to 3
- feedforward_gain: bfloat16 [1536], replicated, may hold values from 0.5 to 1.5
- gate_weight: bfloat16 [4096, 1536], P('fsdp'), may hold values from -0.15625 to 0.15625
- up_weight: bfloat16 [4096, 1536], P('fsdp'), may hold values from -0.15625 to 0.15625
- down_weight: bfloat16 [4096, 1536], P('fsdp'), may hold values from -0.09375 to 0.09375
Outputs:
- layer_output: bfloat16 [4096, 1536], P(('fsdp', 'ctx'))
- input_grad: float32 [4096, 1536], P(('fsdp', 'ctx'))
- attention_gain_grad: float32 [1536], replicated
- query_weight_grad: float32 [1536, 1536], P('fsdp')
- key_weight_grad: float32 [768, 1536], P('fsdp')
- value_weight_grad: float32 [768, 1536], P('fsdp')
- output_weight_grad: float32 [1536, 1536], P('fsdp')
- feedforward_gain_grad: float32 [1536], replicated
- gate_weight_grad: float32 [4096, 1536], P('fsdp')
- up_weight_grad: float32 [4096, 1536], P('fsdp')
- down_weight_grad: float32 [4096, 1536], P('fsdp')
Inputs may be any that keep to these rules, and one draw needn't show every extreme that they name: Within each sequence every position appears once, and each device's 2 * 64 tokens of a sequence are two whole blocks of 64 consecutive rising positions, starting at b * 64 and at (15 - b) * 64 for some b, in either order.
All inputs are finite; a program needn't handle non-finite values.
Results may differ from a plain program's by a relative error of at most 0.022.
Values may be sent and summed in bfloat16 or wider, within the bound.
A program may use at most 384 MiB of HBM per device.

v0:
```python
import math
import jax
import jax.numpy as jnp
from jax import lax
from jax.sharding import PartitionSpec as P

HEADS = 16
KV_HEADS = 8
HEAD_DIM = 96
EPSILON = 1e-05
ROPE_BASE = 100000.0


def product(left, right):
    return jnp.dot(left, right, preferred_element_type=jnp.float32)


def product_back(left, right):
    return lax.dot_general(
        left, right, (((1,), (1,)), ((), ())), preferred_element_type=jnp.float32
    )


def product_rows(left, right):
    return lax.dot_general(
        left, right, (((0,), (0,)), ((), ())), preferred_element_type=jnp.float32
    )


def rms_scale(values):
    return lax.rsqrt(jnp.mean(values * values, axis=-1, keepdims=True) + EPSILON)


def norm_back(scale_rows, unit_rows, grad_unit):
    return scale_rows * (
        grad_unit - unit_rows * jnp.mean(grad_unit * unit_rows, axis=-1, keepdims=True)
    )


def rotary_tables(places):
    half_width = HEAD_DIM // 2
    frequencies = ROPE_BASE ** (-(jnp.arange(half_width, dtype=jnp.float32) * 2.0 / HEAD_DIM))
    angles = places.astype(jnp.float32)[:, None] * frequencies[None, :]
    return (jnp.cos(angles)[:, None, :], jnp.sin(angles)[:, None, :])


def rotate(values, cosine, sine):
    half_width = values.shape[-1] // 2
    lower_half = values[..., :half_width]
    upper_half = values[..., half_width:]
    return jnp.concatenate(
        [lower_half * cosine - upper_half * sine, upper_half * cosine + lower_half * sine], axis=-1
    )


def rotate_back(grads, cosine, sine):
    half_width = grads.shape[-1] // 2
    lower_half = grads[..., :half_width]
    upper_half = grads[..., half_width:]
    return jnp.concatenate(
        [lower_half * cosine + upper_half * sine, upper_half * cosine - lower_half * sine], axis=-1
    )


def block_total_of(total_keys):
    return max(1, total_keys // 512)


def masked_scores(query_grouped, query_places, key_rows, key_places, start, width):
    key_part = lax.dynamic_slice_in_dim(key_rows, start, width, 2)
    place_part = lax.dynamic_slice_in_dim(key_places, start, width, 1)
    scores = jnp.einsum(
        "sqhgd,shkd->shgqk", query_grouped, key_part, preferred_element_type=jnp.float32
    )
    scores = scores * (1.0 / math.sqrt(HEAD_DIM))
    allowed = place_part[:, None, None, None, :] <= query_places[:, None, None, :, None]
    return jnp.where(allowed, scores, -1000000000.0)


def attend_forward(query_grouped, query_places, key_rows, value_rows, key_places):
    seq_count, row_count, head_groups, group_size = query_grouped.shape[:4]
    total_keys = key_rows.shape[2]
    block_total = block_total_of(total_keys)
    width = total_keys // block_total
    stat_shape = (seq_count, head_groups, group_size, row_count)

    def peak_step(index, carry):
        running_top, running_sum = carry
        scores = masked_scores(
            query_grouped, query_places, key_rows, key_places, index * width, width
        )
        new_top = jnp.maximum(running_top, jnp.max(scores, axis=-1))
        running_sum = running_sum * jnp.exp(running_top - new_top) + jnp.sum(
            jnp.exp(scores - new_top[..., None]), axis=-1
        )
        return (new_top, running_sum)

    running_top, running_sum = lax.fori_loop(
        0,
        block_total,
        peak_step,
        (jnp.full(stat_shape, -1e30, jnp.float32), jnp.zeros(stat_shape, jnp.float32)),
    )
    log_total = running_top + jnp.log(running_sum)

    def value_step(index, gathered):
        scores = masked_scores(
            query_grouped, query_places, key_rows, key_places, index * width, width
        )
        soft_low = jnp.exp(scores - log_total[..., None]).astype(jnp.bfloat16)
        value_part = lax.dynamic_slice_in_dim(value_rows, index * width, width, 2)
        return gathered + jnp.einsum(
            "shgqk,shkd->sqhgd", soft_low, value_part, preferred_element_type=jnp.float32
        )

    attended = lax.fori_loop(
        0, block_total, value_step, jnp.zeros(query_grouped.shape, jnp.float32)
    )
    return (attended, log_total)


def attend_backward(
    query_grouped, query_places, key_rows, value_rows, key_places, log_total, grad_attended
):
    total_keys = key_rows.shape[2]
    block_total = block_total_of(total_keys)
    width = total_keys // block_total
    score_scale = 1.0 / math.sqrt(HEAD_DIM)

    def soft_and_grad(index):
        scores = masked_scores(
            query_grouped, query_places, key_rows, key_places, index * width, width
        )
        soft_values = jnp.exp(scores - log_total[..., None])
        value_part = lax.dynamic_slice_in_dim(value_rows, index * width, width, 2)
        grad_soft = jnp.einsum(
            "sqhgd,shkd->shgqk", grad_attended, value_part, preferred_element_type=jnp.float32
        )
        return (soft_values, grad_soft)

    def delta_step(index, row_delta):
        soft_values, grad_soft = soft_and_grad(index)
        return row_delta + jnp.sum(soft_values * grad_soft, axis=-1)

    row_delta = lax.fori_loop(0, block_total, delta_step, jnp.zeros(log_total.shape, jnp.float32))

    def grad_step(index, carry):
        grad_query, grad_keys, grad_values = carry
        soft_values, grad_soft = soft_and_grad(index)
        grad_scores = (soft_values * (grad_soft - row_delta[..., None])).astype(jnp.bfloat16)
        key_part = lax.dynamic_slice_in_dim(key_rows, index * width, width, 2)
        grad_query = (
            grad_query
            + jnp.einsum(
                "shgqk,shkd->sqhgd", grad_scores, key_part, preferred_element_type=jnp.float32
            )
            * score_scale
        )
        key_term = (
            jnp.einsum(
                "shgqk,sqhgd->shkd", grad_scores, query_grouped, preferred_element_type=jnp.float32
            )
            * score_scale
        )
        value_term = jnp.einsum(
            "shgqk,sqhgd->shkd",
            soft_values.astype(jnp.bfloat16),
            grad_attended,
            preferred_element_type=jnp.float32,
        )
        grad_keys = lax.dynamic_update_slice_in_dim(grad_keys, key_term, index * width, 2)
        grad_values = lax.dynamic_update_slice_in_dim(grad_values, value_term, index * width, 2)
        return (grad_query, grad_keys, grad_values)

    initial = (
        jnp.zeros(query_grouped.shape, jnp.float32),
        jnp.zeros(key_rows.shape, jnp.float32),
        jnp.zeros(value_rows.shape, jnp.float32),
    )
    return lax.fori_loop(0, block_total, grad_step, initial)


def gather_rows(values):
    return lax.all_gather(values, "fsdp", axis=0, tiled=True)


def scatter_rows(values):
    return lax.psum_scatter(
        values.astype(jnp.bfloat16), "fsdp", scatter_dimension=0, tiled=True
    ).astype(jnp.float32)


def per_device(
    inputs,
    positions,
    cotangent,
    attention_gain,
    query_weight,
    key_weight,
    value_weight,
    output_weight,
    feedforward_gain,
    gate_weight,
    up_weight,
    down_weight,
):
    row_count = inputs.shape[0]
    groups = HEADS // KV_HEADS
    gain_one = attention_gain.astype(jnp.float32)
    gain_two = feedforward_gain.astype(jnp.float32)
    seq_count = lax.axis_size("fsdp")
    first_row = lax.axis_index("fsdp") * row_count

    def own(values):
        return lax.dynamic_slice_in_dim(values, first_row, row_count, 0)

    query_places = gather_rows(positions).reshape(seq_count, row_count)
    key_places = lax.all_gather(query_places, "ctx", axis=1, tiled=True)
    all_cotangent = gather_rows(cotangent)
    flat_in = gather_rows(inputs).astype(jnp.float32)
    scale_one = rms_scale(flat_in)
    unit_one = flat_in * scale_one
    normed_one = (unit_one * gain_one).astype(jnp.bfloat16)
    total_rows = normed_one.shape[0]
    cosine, sine = rotary_tables(query_places.reshape(-1))
    query_heads = query_weight.shape[0] // HEAD_DIM
    kv_heads = key_weight.shape[0] // HEAD_DIM
    kv_width = kv_heads * HEAD_DIM
    query_low = rotate(
        product_back(normed_one, query_weight).reshape(total_rows, query_heads, HEAD_DIM),
        cosine,
        sine,
    ).astype(jnp.bfloat16)
    key_low = rotate(
        product_back(normed_one, key_weight).reshape(total_rows, kv_heads, HEAD_DIM), cosine, sine
    ).astype(jnp.bfloat16)
    value_low = product_back(normed_one, value_weight).astype(jnp.bfloat16)
    ctx_size = lax.axis_size("ctx")

    def spread(values):
        rows = lax.all_gather(values, "ctx", axis=0, tiled=True)
        rows = rows.reshape(ctx_size, seq_count, row_count, kv_width).swapaxes(0, 1)
        return rows.reshape(seq_count, ctx_size * row_count, kv_width)

    def collect(values):
        rows = values.astype(jnp.bfloat16).swapaxes(1, 2)
        rows = rows.reshape(seq_count, ctx_size, row_count, kv_width).swapaxes(0, 1)
        return lax.psum_scatter(rows.reshape(-1, kv_width), "ctx", scatter_dimension=0, tiled=True)

    all_keys = spread(key_low.reshape(total_rows, kv_width))
    all_values = spread(value_low)
    total_keys = all_keys.shape[1]
    key_grid = all_keys.reshape(seq_count, total_keys, kv_heads, HEAD_DIM).swapaxes(1, 2)
    value_grid = all_values.reshape(seq_count, total_keys, kv_heads, HEAD_DIM).swapaxes(1, 2)
    query_grouped = query_low.reshape(seq_count, row_count, kv_heads, groups, HEAD_DIM)
    attended, log_total = attend_forward(
        query_grouped, query_places, key_grid, value_grid, key_places
    )
    attended_low = attended.reshape(total_rows, query_heads * HEAD_DIM).astype(jnp.bfloat16)
    hidden_state = inputs.astype(jnp.float32) + scatter_rows(product(attended_low, output_weight))
    scale_two = rms_scale(hidden_state)
    unit_two = hidden_state * scale_two
    normed_two = gather_rows((unit_two * gain_two).astype(jnp.bfloat16))
    gate_values = product_back(normed_two, gate_weight)
    upward = product_back(normed_two, up_weight)
    sigmoid_gate = jax.nn.sigmoid(gate_values)
    activated = gate_values * sigmoid_gate
    mixed_hidden = (activated * upward).astype(jnp.bfloat16)
    grad_out = cotangent.astype(jnp.float32)
    grad_down = product_rows(mixed_hidden, all_cotangent)
    grad_mixed = product_back(all_cotangent, down_weight)
    grad_gate_low = (
        grad_mixed * upward * sigmoid_gate * (1.0 + gate_values * (1.0 - sigmoid_gate))
    ).astype(jnp.bfloat16)
    grad_up_low = (grad_mixed * activated).astype(jnp.bfloat16)
    grad_normed_two = scatter_rows(
        product(grad_gate_low, gate_weight) + product(grad_up_low, up_weight)
    )
    gain_two_grad = jnp.sum(grad_normed_two * unit_two, axis=0)
    grad_hidden = grad_out + norm_back(scale_two, unit_two, grad_normed_two * gain_two)
    branch_rows = gather_rows(grad_hidden.astype(jnp.bfloat16))
    layer_output = (hidden_state + scatter_rows(product(mixed_hidden, down_weight))).astype(
        jnp.bfloat16
    )
    grad_gate = product_rows(grad_gate_low, normed_two)
    grad_up = product_rows(grad_up_low, normed_two)
    grad_output = product_rows(attended_low, branch_rows)
    grad_attended = product_back(branch_rows, output_weight).astype(jnp.bfloat16)
    grad_attended = grad_attended.reshape(seq_count, row_count, kv_heads, groups, HEAD_DIM)
    grad_query_rot, grad_key_all, grad_value_all = attend_backward(
        query_grouped, query_places, key_grid, value_grid, key_places, log_total, grad_attended
    )
    grad_key_own = collect(grad_key_all).astype(jnp.float32)
    grad_value_low = collect(grad_value_all)
    grad_query_low = (
        rotate_back(grad_query_rot.reshape(total_rows, query_heads, HEAD_DIM), cosine, sine)
        .reshape(total_rows, query_heads * HEAD_DIM)
        .astype(jnp.bfloat16)
    )
    grad_key_low = (
        rotate_back(grad_key_own.reshape(total_rows, kv_heads, HEAD_DIM), cosine, sine)
        .reshape(total_rows, kv_width)
        .astype(jnp.bfloat16)
    )
    grad_query = product_rows(grad_query_low, normed_one)
    grad_key = product_rows(grad_key_low, normed_one)
    grad_value = product_rows(grad_value_low, normed_one)
    grad_normed_one = scatter_rows(
        product(grad_query_low, query_weight)
        + product(grad_key_low, key_weight)
        + product(grad_value_low, value_weight)
    )
    own_unit = own(unit_one)
    gain_one_grad = jnp.sum(grad_normed_one * own_unit, axis=0)
    input_grad = grad_hidden + norm_back(own(scale_one), own_unit, grad_normed_one * gain_one)

    def ctx_sum(grad):
        return lax.psum(grad.astype(jnp.bfloat16), "ctx").astype(jnp.float32)

    gain_sums = lax.psum(jnp.stack([gain_one_grad, gain_two_grad]), ("fsdp", "ctx"))
    return (
        layer_output,
        input_grad,
        gain_sums[0],
        ctx_sum(grad_query),
        ctx_sum(grad_key),
        ctx_sum(grad_value),
        ctx_sum(grad_output),
        gain_sums[1],
        ctx_sum(grad_gate),
        ctx_sum(grad_up),
        ctx_sum(grad_down),
    )


def solution(mesh):
    in_specs = (
        P(("fsdp", "ctx"), None),
        P(("fsdp", "ctx")),
        P(("fsdp", "ctx"), None),
        P(),
        P("fsdp", None),
        P("fsdp", None),
        P("fsdp", None),
        P("fsdp", None),
        P(),
        P("fsdp", None),
        P("fsdp", None),
        P("fsdp", None),
    )
    out_specs = (
        P(("fsdp", "ctx"), None),
        P(("fsdp", "ctx"), None),
        P(),
        P("fsdp", None),
        P("fsdp", None),
        P("fsdp", None),
        P("fsdp", None),
        P(),
        P("fsdp", None),
        P("fsdp", None),
        P("fsdp", None),
    )
    return jax.shard_map(
        per_device, mesh=mesh, in_specs=in_specs, out_specs=out_specs, check_vma=False
    )
```

profile of v0, /device:TPU:0, one launch (start us, length us, event | category | flops | bytes accessed | tf_op | source)
XLA Modules:
  0.0 985.5 jit_solution(4520594425977909812)
XLA Ops:
  8.8 6.2 all-gather
  15.5 16.5 %all-gather.8.cloned.1.call-done = bf16[512,1536]{1,0:T(8,128)(2,1)} async-done(((bf16[128,1536]{1,0:T(8,128)(2,1)}), bf16[512,1536]{1,0:T(8,128)(2,1)}) %all-gather.8.cloned.1.call-update) | async-done | bytes 1572880 | tf_op jit(solution)/shard_map/all_gather | solution.py:184
  36.9 26.4 %all_gather.27 = s32[4,1024]{1,0:T(4,128)S(1)} all-gather(s32[4,128]{1,0:T(4,128)S(1)} %bitcast.305), channel_id=1, replica_groups=mesh['fsdp'=4,'ctx'=8] {'ctx'}, dimensions={1}, use_global_device_ids=true | all-gather | bytes 18432 | tf_op jit(solution)/shard_map/all_gather | solution.py:218
  71.2 10.2 %all-gather.12.cloned.1.call-done = bf16[4096,192]{0,1:T(8,128)(2,1)} async-done(((bf16[512,192]{0,1:T(8,128)(2,1)}), bf16[4096,192]{0,1:T(8,128)(2,1)}) %all-gather.12.cloned.1.call-update) | async-done | bytes 1572880 | tf_op jit(solution)/shard_map/all_gather | solution.py:241
  81.4 3.8 reshape.215
  91.7 20.6 %while.62 = (s32[]{:T(128)}, f32[4,2,2,128]{3,2,1,0:T(2,128)}, f32[4,2,2,128]{3,2,1,0:T(2,128)}, s32[4,1024]{1,0:T(4,128)S(1)}, s32[512]{0:T(512)}, /*index=5*/b...) while((s32[]{:T(128)}, f32[4,2,2,128]{3,2,1,0:T(2,128)}, ...), condition=%wide.region_4.5_spmd.clone, body=%wide.region_1.4_spmd.clone.sunk | while | flops 208939008 | bytes 11634982 | solution.py:98
  92.8 4.7 fusion.162
  103.0 4.7 fusion.162
  112.3 14.3 %all-gather.10.cloned.1.call-done = bf16[4096,192]{0,1:T(8,128)(2,1)} async-done(((bf16[512,192]{0,1:T(8,128)(2,1)}), bf16[4096,192]{0,1:T(8,128)(2,1)}) %all-gather.10.cloned.1.call-update) | async-done | bytes 1572880 | tf_op jit(solution)/shard_map/all_gather | solution.py:241
  126.6 3.8 reshape.212
  138.2 11.5 %while.63 = (s32[]{:T(128)}, f32[4,128,2,2,96]{1,4,3,2,0:T(8,128)}, bf16[4,2,1024,96]{2,3,1,0:T(8,128)(2,1)}, s32[4,1024]{1,0:T(4,128)S(1)}, s32[512]{0:T(512)},...) while((s32[]{:T(128)}, f32[4,128,2,2,96]{1,4,3,2,0:T(8,128)}, ...), condition=%wide.region_6.7_spmd.clone, body=%wide.region_5.6_spmd.clone.sunk | while | flops 407502848 | bytes 4099768 | solution.py:116
  139.9 3.9 fusion.168
  145.5 4.1 fusion.168
  156.7 25.1 %reduce-scatter.7.cloned.1.call-done = bf16[128,1536]{1,0:T(8,128)(2,1)} async-done(((bf16[512,1536]{1,0:T(8,128)(2,1)}), bf16[128,1536]{1,0:T(8,128)(2,1)}) %reduce-scatter.7.cloned.1.call-update) | async-done | bytes 393232 | tf_op jit(solution)/shard_map/reduce_scatter | solution.py:188
  186.5 19.0 %all-gather.14.cloned.1.call-done = bf16[512,1536]{1,0:T(8,128)(2,1)} async-done(((bf16[128,1536]{1,0:T(8,128)(2,1)}), bf16[512,1536]{1,0:T(8,128)(2,1)}) %all-gather.14.cloned.1.call-update) | async-done | bytes 1572880 | tf_op jit(solution)/shard_map/all_gather | solution.py:184
  205.5 5.6 fusion.85
  214.3 12.3 %all-gather.16.cloned.1.call-done = bf16[512,1536]{1,0:T(8,128)(2,1)} async-done(((bf16[128,1536]{1,0:T(8,128)(2,1)}), bf16[512,1536]{1,0:T(8,128)(2,1)}) %all-gather.16.cloned.1.call-update) | async-done | bytes 1572880 | tf_op jit(solution)/shard_map/all_gather | solution.py:184
  226.6 6.3 multiply_convert_fusion.1
  238.6 28.1 %reduce-scatter.11.cloned.1.call-done = bf16[128,1536]{1,0:T(8,128)(2,1)} async-done(((bf16[512,1536]{1,0:T(8,128)(2,1)}), bf16[128,1536]{1,0:T(8,128)(2,1)}) %reduce-scatter.11.cloned.1.call-update) | async-done | bytes 393232 | tf_op jit(solution)/shard_map/reduce_scatter | solution.py:188
  272.2 19.5 %all-gather.18.cloned.1.call-done = bf16[512,1536]{1,0:T(8,128)(2,1)} async-done(((bf16[128,1536]{1,0:T(8,128)(2,1)}), bf16[512,1536]{1,0:T(8,128)(2,1)}) %all-gather.18.cloned.1.call-update) | async-done | bytes 1572880 | tf_op jit(solution)/shard_map/all_gather | solution.py:184
  299.2 11.5 %while.64 = (s32[]{:T(128)}, f32[4,2,2,128]{3,2,1,0:T(2,128)}, s32[4,1024]{1,0:T(4,128)S(1)}, s32[512]{0:T(512)}, bf16[4,2,1024,96]{2,3,1,0:T(8,128)(2,1)}, /*in...) while((s32[]{:T(128)}, f32[4,2,2,128]{3,2,1,0:T(2,128)}, ...), condition=%wide.region_14.0_spmd.clone, body=%wide.region_12.0_spmd.clone.sunk | while | flops 408160256 | bytes 19245368 | solution.py:145
  313.5 29.0 %while.65 = (s32[]{:T(128)}, f32[4,128,2,2,96]{1,4,3,2,0:T(8,128)}, bf16[4,2,1024,96]{2,3,1,0:T(8,128)(2,1)}, bf16[4,2,1024,96]{2,3,1,0:T(8,128)(2,1)}, bf16[4,2...) while((s32[]{:T(128)}, f32[4,128,2,2,96]{1,4,3,2,0:T(8,128)}, ...), condition=%wide.region_16.17_spmd.clone, body=%wide.region_15.16_spmd.clone.sunk | while | flops 1018363904 | bytes 86141536 | solution.py:180
  347.5 3.8 reshape.220
  356.9 3.8 reshape.224
  369.8 47.8 %reduce-scatter.13.cloned.1.call-done = bf16[512,192]{0,1:T(8,128)(2,1)} async-done(((bf16[4096,192]{0,1:T(8,128)(2,1)}), bf16[512,192]{0,1:T(8,128)(2,1)}) %reduce-scatter.13.cloned.1.call-update) | async-done | bytes 196624 | tf_op jit(solution)/shard_map/reduce_scatter | solution.py:248
  420.4 4.2 convolution_add_fusion.1
  424.6 62.0 %reduce-scatter.15.cloned.1.call-done = bf16[512,192]{0,1:T(8,128)(2,1)} async-done(((bf16[4096,192]{0,1:T(8,128)(2,1)}), bf16[512,192]{0,1:T(8,128)(2,1)}) %reduce-scatter.15.cloned.1.call-update) | async-done | bytes 196624 | tf_op jit(solution)/shard_map/reduce_scatter | solution.py:248
  486.6 3.9 fusion.63
  490.5 4.2 convolution_convert_fusion.3
  495.0 5.5 convolution_convert_fusion.2
  522.3 39.8 %psum.56 = f32[2,1536]{1,0:T(2,128)} all-reduce(f32[2,1536]{1,0:T(2,128)} %pad_maximum_fusion.4), channel_id=1, replica_groups=mesh['fsdp'=4,'ctx'=8] {'fsdp','ctx'}, use_global_device_ids=true, to_apply=%region_23.24 | all-reduce | flops 3072 | bytes 24576 | tf_op jit(solution)/shard_map/psum | solution.py:320
  567.8 392.1 %all-reduce.3.cloned.1.call-done = (bf16[384,1536]{1,0:T(8,128)(2,1)}, bf16[192,1536]{1,0:T(8,128)(2,1)}, bf16[192,1536]{1,0:T(8,128)(2,1)}, bf16[384,1536]{1,0:...) async-done(((bf16[384,1536]{1,0:T(8,128)(2,1)}, bf16[192,1536]{1,0:T(8,128)(2,1)}, bf16[192,1536]{1,0:T(8,128)(2,1)}, ...) | async-done | bytes 12976144 | tf_op jit(solution)/shard_map/psum | solution.py:318
  (310 shorter events, 188.9 us)
Async XLA Ops:
  7.2 219.5 %copy-start = (bf16[1024,1536]{1,0:T(8,128)(2,1)S(1)}, bf16[1024,1536]{1,0:T(8,128)(2,1)}, u32[]{:S(2)}) copy-start(bf16[1024,1536]{1,0:T(8,128)(2,1)} %param.31) | copy-start | bytes 9437188
  7.2 24.8 %all-gather.8.cloned.1.call-start = ((), (), s32[]{:S(2)}) async-start(), calls=%async_computation.6 | async-start | bytes 1966080 | tf_op jit(solution)/shard_map/all_gather | solution.py:184
  7.9 73.5 %all-gather.12.cloned.1.call-start = ((), (), s32[]{:S(2)}) async-start(), calls=%async_computation.8 | async-start | bytes 1769472 | tf_op jit(solution)/shard_map/all_gather | solution.py:241
  8.8 54.5 %copy-start.40 = (f32[1536]{0:T(1024)}, f32[1536]{0:T(1024)S(1)}, u32[]{:S(2)}) copy-start(f32[1536]{0:T(1024)S(1)} %convert_element_type.162) | copy-start | bytes 18436
  15.0 21.9 %copy-start.23 = (s32[4,1,128]{2,1,0:T(1,128)}, s32[4,1,128]{2,1,0:T(1,128)S(1)}, u32[]{:S(2)}) copy-start(s32[4,1,128]{2,1,0:T(1,128)S(1)} %all-gather) | copy-start | bytes 6148
  15.5 50.5 %copy-start.13 = (f32[512,48]{0,1:T(8,128)}, f32[512,48]{0,1:T(8,128)S(1)}, u32[]{:S(2)}) copy-start(f32[512,48]{0,1:T(8,128)S(1)} %get-tuple-element.994) | copy-start | bytes 294916
  15.5 50.5 %copy-start.15 = (f32[512,48]{0,1:T(8,128)}, f32[512,48]{0,1:T(8,128)S(1)}, u32[]{:S(2)}) copy-start(f32[512,48]{0,1:T(8,128)S(1)} %get-tuple-element.995) | copy-start | bytes 294916
  33.7 29.5 %copy-start.44 = (f32[512]{0:T(512)}, f32[512]{0:T(512)S(1)}, u32[]{:S(2)}) copy-start(f32[512]{0:T(512)S(1)} %add_rsqrt_fusion) | copy-start | bytes 6148
  36.8 89.8 %all-gather.10.cloned.1.call-start = ((), (), s32[]{:S(2)}) async-start(), calls=%async_computation.7 | async-start | bytes 1769472 | tf_op jit(solution)/shard_map/all_gather | solution.py:241
  71.2 110.6 %reduce-scatter.7.cloned.1.call-start = ((), (), s32[]{:S(2)}) async-start(), calls=%async_computation.9 | async-start | bytes 1966080 | tf_op jit(solution)/shard_map/reduce_scatter | solution.py:188
  92.8 4.7 copy-start.3
  103.0 4.7 copy-start.3
  155.4 50.1 %all-gather.14.cloned.1.call-start = ((), (), s32[]{:S(2)}) async-start(), calls=%async_computation.10 | async-start | bytes 1966080 | tf_op jit(solution)/shard_map/all_gather | solution.py:184
  185.7 40.9 %all-gather.16.cloned.1.call-start = ((), (), s32[]{:S(2)}) async-start(), calls=%async_computation.12 | async-start | bytes 1966080 | tf_op jit(solution)/shard_map/all_gather | solution.py:184
  186.3 80.4 %reduce-scatter.11.cloned.1.call-start = ((), (), s32[]{:S(2)}) async-start(), calls=%async_computation.13 | async-start | bytes 1966080 | tf_op jit(solution)/shard_map/reduce_scatter | solution.py:188
  205.5 5.7 copy-start.51
  205.5 5.7 copy-start.53
  226.6 6.3 copy-start.50
  238.6 53.1 %all-gather.18.cloned.1.call-start = ((), (), s32[]{:S(2)}) async-start(), calls=%async_computation.14 | async-start | bytes 1966080 | tf_op jit(solution)/shard_map/all_gather | solution.py:184
  271.9 145.8 %reduce-scatter.13.cloned.1.call-start = ((), (), s32[]{:S(2)}) async-start(), calls=%async_computation.15 | async-start | bytes 1769472 | tf_op jit(solution)/shard_map/reduce_scatter | solution.py:248
  318.8 6.8 copy-start.2
  333.2 6.9 copy-start.2
  351.4 135.2 %reduce-scatter.15.cloned.1.call-start = ((), (), s32[]{:S(2)}) async-start(), calls=%async_computation.16 | async-start | bytes 1769472 | tf_op jit(solution)/shard_map/reduce_scatter | solution.py:248
  360.7 5.0 copy-start.14
  360.7 5.0 copy-start.16
  360.7 158.2 %reduce-scatter.17.cloned.1.call-start = ((), (), s32[]{:S(2)}) async-start(), calls=%async_computation.17 | async-start | bytes 1966080 | tf_op jit(solution)/shard_map/reduce_scatter | solution.py:188
  490.5 74.2 %reduce-scatter.9.cloned.1.call-start = ((), (), s32[]{:S(2)}) async-start(), calls=%async_computation.11 | async-start | bytes 1966080 | tf_op jit(solution)/shard_map/reduce_scatter | solution.py:188
  494.7 465.2 %all-reduce.3.cloned.1.call-start = ((), (), s32[]{:S(2)}) async-start(), calls=%async_computation.18 | async-start | bytes 25952256 | tf_op jit(solution)/shard_map/psum | solution.py:318
  495.0 5.6 copy-start.54
  495.0 5.6 copy-start.58
  514.9 49.8 %copy-start.4 = (bf16[128,1536]{1,0:T(8,128)(2,1)S(1)}, bf16[128,1536]{1,0:T(8,128)(2,1)}, u32[]{:S(2)}) copy-start(bf16[128,1536]{1,0:T(8,128)(2,1)} %param.20) | copy-start | bytes 1179652
  514.9 49.8 %copy-start.37 = (f32[1536]{0:T(1024)S(1)}, f32[1536]{0:T(1024)}, u32[]{:S(2)}) copy-start(f32[1536]{0:T(1024)} %convert_element_type.171) | copy-start | bytes 18436
  (63 other events, 157.4 us)
Sparse Core Ops, SparseCore 0:
  9.6 22.3 all-gather.7
  37.0 44.4 all-gather.11
  84.1 42.5 all-gather.9
  155.5 26.2 reduce-scatter.6
  185.8 19.6 all-gather.13
  206.9 19.6 all-gather.15
  238.7 27.9 reduce-scatter.10
  272.0 19.6 all-gather.17
  351.5 66.1 reduce-scatter.12
  421.5 65.0 reduce-scatter.14
  490.6 26.7 reduce-scatter.16
  520.4 27.9 reduce-scatter.8
  555.3 404.5 all-reduce.2
where the time goes:
time: 996 us; the launch traced here: 985 us
  waiting for transfers between devices  648 us (65%)
  matrix products  120 us (12%)
  blocking collectives  72.3 us (7%)
  other arithmetic  66.2 us (7%)
  local copies, waits for them, and re-layouts  62.1 us (6%)
  between operations  14.5 us (1%)
    psum x1, waiting for transfers between devices, ctx_sum(): return lax.psum(grad.astype(jnp.bfloat16), 'ctx').astype(jnp.float32)  392 us
    reduce_scatter x2, waiting for transfers between devices, collect(): lax.psum_scatter(rows.reshape(-1, kv_width), 'ctx', scatter_dimension=0,...  110 us
    all_gather x4, waiting for transfers between devices, gather_rows(): return lax.all_gather(values, 'fsdp', axis=0, tiled=True)  67.3 us
    reduce_scatter x4, waiting for transfers between devices, scatter_rows(): lax.psum_scatter(values.astype(jnp.bfloat16), 'fsdp', scatter_dimension=0...  53.2 us
    psum x1, blocking collectives, per_device(): lax.psum(jnp.stack([gain_one_grad, gain_two_grad]), ('fsdp', 'ctx'))  39.8 us
    dot_general x7, matrix products, product_back(): lax.dot_general(left, right, (((1,), (1,)), ((), ())), preferred_element_...  26.5 us
    all_gather x1, blocking collectives, per_device(): key_places = lax.all_gather(query_places, 'ctx', axis=1, tiled=True)  26.4 us
    all_gather x2, waiting for transfers between devices, spread(): rows = lax.all_gather(values, 'ctx', axis=0, tiled=True)  24.5 us
  transfers between devices with their start and end apart: 13, of which 11 were waited for; matrix products, arithmetic and copies ran while one was open for 11% of the time, Pallas kernels for 0%

commit v1 on v0

--- a/solution.py
+++ b/solution.py
@@ -9,6 +9,27 @@
 HEAD_DIM = 96
 EPSILON = 1e-05
 ROPE_BASE = 100000.0
+
+
+def ring_gather(value, axis, dim):
+    devices, place, extent = (lax.axis_size(axis), lax.axis_index(axis), value.shape[dim])
+    forward = [(i, (i + 1) % devices) for i in range(devices)]
+    left = [(i, (i - 1) % devices) for i in range(devices)]
+    out = jnp.zeros((*value.shape[:dim], devices * extent, *value.shape[dim + 1 :]), value.dtype)
+    out = lax.dynamic_update_slice_in_dim(out, value, place * extent, axis=dim)
+    from_left = from_right = value
+    half = devices // 2
+    for step in range(1, half + 1):
+        from_left = lax.ppermute(from_left, axis, forward)
+        out = lax.dynamic_update_slice_in_dim(
+            out, from_left, (place - step) % devices * extent, axis=dim
+        )
+        if step < devices - half:
+            from_right = lax.ppermute(from_right, axis, left)
+            out = lax.dynamic_update_slice_in_dim(
+                out, from_right, (place + step) % devices * extent, axis=dim
+            )
+    return out
 
 
 def product(left, right):
@@ -238,7 +259,7 @@
     ctx_size = lax.axis_size("ctx")
 
     def spread(values):
-        rows = lax.all_gather(values, "ctx", axis=0, tiled=True)
+        rows = ring_gather(values, "ctx", 0)
         rows = rows.reshape(ctx_size, seq_count, row_count, kv_width).swapaxes(0, 1)
         return rows.reshape(seq_count, ctx_size * row_count, kv_width)
 

time: 996 us -> 1010 us (1.014)
  waiting for transfers between devices: 648 us -> 613 us
  starting transfers between devices: 1.49 us -> 35.7 us
  local copies, waits for them, and re-layouts: 62.1 us -> 79.2 us
    ppermute x0 -> x14, starting transfers between devices: none -> 34.2 us  [the longest x6 25 us: ring_gather(): from_right = lax.ppermute(from_right, axis, left)]
    all_gather x2 -> x0, waiting for transfers between devices: 24.5 us -> none  [spread(): rows = lax.all_gather(values, 'ctx', axis=0, tiled=True)]
    all_gather x4, waiting for transfers between devices: 67.3 us -> 50.8 us  [gather_rows(): return lax.all_gather(values, 'fsdp', axis=0, tiled=True)]
    dynamic_update_slice x0 -> x14, local copies, waits for them, and re-layouts: none -> 14.4 us  [the longest x7 6.75 us: ring_gather(): lax.dynamic_update_slice_in_dim(out, from_left, (place - step) % devices...]
  transfers between devices with their start and end apart: 13 -> 25, of which waited for: 11 -> 12; matrix products, arithmetic and copies ran while one was open for 11% -> 9% of each run, Pallas kernels for 0% -> 0%
where the time goes in v1:
time: 1010 us; the launch traced here: 999 us
  waiting for transfers between devices  613 us (61%)
  matrix products  117 us (12%)
  local copies, waits for them, and re-layouts  79.2 us (8%)
  blocking collectives  72.9 us (7%)
  other arithmetic  66 us (7%)
  starting transfers between devices  35.7 us (4%)
  between operations  14.6 us (1%)
    psum x1, waiting for transfers between devices, ctx_sum(): return lax.psum(grad.astype(jnp.bfloat16), 'ctx').astype(jnp.float32)  392 us
    reduce_scatter x2, waiting for transfers between devices, collect(): lax.psum_scatter(rows.reshape(-1, kv_width), 'ctx', scatter_dimension=0,...  110 us
    reduce_scatter x4, waiting for transfers between devices, scatter_rows(): lax.psum_scatter(values.astype(jnp.bfloat16), 'fsdp', scatter_dimension=0...  53.7 us
    all_gather x4, waiting for transfers between devices, gather_rows(): return lax.all_gather(values, 'fsdp', axis=0, tiled=True)  50.8 us
    psum x1, blocking collectives, per_device(): lax.psum(jnp.stack([gain_one_grad, gain_two_grad]), ('fsdp', 'ctx'))  39.8 us
    all_gather x1, blocking collectives, per_device(): key_places = lax.all_gather(query_places, 'ctx', axis=1, tiled=True)  26.9 us
    ppermute x6, starting transfers between devices, ring_gather(): from_right = lax.ppermute(from_right, axis, left)  25 us
    dot_general x7, matrix products, product_back(): lax.dot_general(left, right, (((1,), (1,)), ((), ())), preferred_element_...  23.2 us
  transfers between devices with their start and end apart: 25, of which 12 were waited for; matrix products, arithmetic and copies ran while one was open for 9% of the time, Pallas kernels for 0%

profile of v1, /device:TPU:0, one launch (start us, length us, event | category | flops | bytes accessed | tf_op | source)
XLA Modules:
  0.0 999.0 jit_solution(17784719770986476142)
XLA Ops:
  8.8 6.2 all-gather
  15.0 26.9 %all_gather.20 = s32[4,1024]{1,0:T(4,128)S(1)} all-gather(s32[4,128]{1,0:T(4,128)S(1)} %bitcast.305), channel_id=1, replica_groups=mesh['fsdp'=4,'ctx'=8] {'ctx'}, dimensions={1}, use_global_device_ids=true | all-gather | bytes 18432 | tf_op jit(solution)/shard_map/all_gather | solution.py:239
  54.9 4.7 collective-permute-start.1
  65.7 4.7 collective-permute-start.10
  73.7 4.7 collective-permute-start.3
  81.6 4.7 collective-permute-start.12
  119.1 20.5 %while.62 = (s32[]{:T(128)}, f32[4,2,2,128]{3,2,1,0:T(2,128)}, f32[4,2,2,128]{3,2,1,0:T(2,128)}, s32[4,1024]{1,0:T(4,128)S(1)}, s32[512]{0:T(512)}, /*index=5*/b...) while((s32[]{:T(128)}, f32[4,2,2,128]{3,2,1,0:T(2,128)}, ...), condition=%wide.region_4.5_spmd.clone, body=%wide.region_1.4_spmd.clone.sunk | while | flops 208939008 | bytes 11634982 | solution.py:119
  120.1 4.7 fusion.162
  130.3 4.7 fusion.162
  139.6 3.8 reshape.212
  151.1 11.4 %while.63 = (s32[]{:T(128)}, f32[4,128,2,2,96]{1,4,3,2,0:T(8,128)}, bf16[4,2,1024,96]{2,3,1,0:T(8,128)(2,1)}, s32[4,1024]{1,0:T(4,128)S(1)}, s32[512]{0:T(512)},...) while((s32[]{:T(128)}, f32[4,128,2,2,96]{1,4,3,2,0:T(8,128)}, ...), condition=%wide.region_6.7_spmd.clone, body=%wide.region_5.6_spmd.clone.sunk | while | flops 407502848 | bytes 4099768 | solution.py:137
  152.8 3.9 fusion.168
  158.4 4.1 fusion.168
  169.6 25.6 %reduce-scatter.7.cloned.1.call-done = bf16[128,1536]{1,0:T(8,128)(2,1)} async-done(((bf16[512,1536]{1,0:T(8,128)(2,1)}), bf16[128,1536]{1,0:T(8,128)(2,1)}) %reduce-scatter.7.cloned.1.call-update) | async-done | bytes 393232 | tf_op jit(solution)/shard_map/reduce_scatter | solution.py:209
  199.9 19.0 %all-gather.8.cloned.1.call-done = bf16[512,1536]{1,0:T(8,128)(2,1)} async-done(((bf16[128,1536]{1,0:T(8,128)(2,1)}), bf16[512,1536]{1,0:T(8,128)(2,1)}) %all-gather.8.cloned.1.call-update) | async-done | bytes 1572880 | tf_op jit(solution)/shard_map/all_gather | solution.py:205
  218.9 5.6 fusion.85
  227.7 12.3 %all-gather.10.cloned.1.call-done = bf16[512,1536]{1,0:T(8,128)(2,1)} async-done(((bf16[128,1536]{1,0:T(8,128)(2,1)}), bf16[512,1536]{1,0:T(8,128)(2,1)}) %all-gather.10.cloned.1.call-update) | async-done | bytes 1572880 | tf_op jit(solution)/shard_map/all_gather | solution.py:205
  240.1 6.3 multiply_convert_fusion.1
  252.0 28.1 %reduce-scatter.11.cloned.1.call-done = bf16[128,1536]{1,0:T(8,128)(2,1)} async-done(((bf16[512,1536]{1,0:T(8,128)(2,1)}), bf16[128,1536]{1,0:T(8,128)(2,1)}) %reduce-scatter.11.cloned.1.call-update) | async-done | bytes 393232 | tf_op jit(solution)/shard_map/reduce_scatter | solution.py:209
  285.6 19.5 %all-gather.12.cloned.1.call-done = bf16[512,1536]{1,0:T(8,128)(2,1)} async-done(((bf16[128,1536]{1,0:T(8,128)(2,1)}), bf16[512,1536]{1,0:T(8,128)(2,1)}) %all-gather.12.cloned.1.call-update) | async-done | bytes 1572880 | tf_op jit(solution)/shard_map/all_gather | solution.py:205
  312.7 11.5 %while.64 = (s32[]{:T(128)}, f32[4,2,2,128]{3,2,1,0:T(2,128)}, s32[4,1024]{1,0:T(4,128)S(1)}, s32[512]{0:T(512)}, bf16[4,2,1024,96]{2,3,1,0:T(8,128)(2,1)}, /*in...) while((s32[]{:T(128)}, f32[4,2,2,128]{3,2,1,0:T(2,128)}, ...), condition=%wide.region_14.15_spmd.clone, body=%wide.region_12.14_spmd.clone.sunk | while | flops 408160256 | bytes 19245368 | solution.py:166
  326.9 29.0 %while.65 = (s32[]{:T(128)}, f32[4,128,2,2,96]{1,4,3,2,0:T(8,128)}, bf16[4,2,1024,96]{2,3,1,0:T(8,128)(2,1)}, bf16[4,2,1024,96]{2,3,1,0:T(8,128)(2,1)}, bf16[4,2...) while((s32[]{:T(128)}, f32[4,128,2,2,96]{1,4,3,2,0:T(8,128)}, ...), condition=%wide.region_16.17_spmd.clone, body=%wide.region_15.16_spmd.clone.sunk | while | flops 1018363904 | bytes 86141536 | solution.py:201
  361.0 3.8 reshape.220
  370.3 3.8 reshape.224
  383.3 47.8 %reduce-scatter.13.cloned.1.call-done = bf16[512,192]{0,1:T(8,128)(2,1)} async-done(((bf16[4096,192]{0,1:T(8,128)(2,1)}), bf16[512,192]{0,1:T(8,128)(2,1)}) %reduce-scatter.13.cloned.1.call-update) | async-done | bytes 196624 | tf_op jit(solution)/shard_map/reduce_scatter | solution.py:269
  433.8 4.2 convolution_add_fusion.1
  438.0 62.1 %reduce-scatter.15.cloned.1.call-done = bf16[512,192]{0,1:T(8,128)(2,1)} async-done(((bf16[4096,192]{0,1:T(8,128)(2,1)}), bf16[512,192]{0,1:T(8,128)(2,1)}) %reduce-scatter.15.cloned.1.call-update) | async-done | bytes 196624 | tf_op jit(solution)/shard_map/reduce_scatter | solution.py:269
  500.1 3.9 fusion.63
  504.1 4.2 convolution_convert_fusion.3
  508.5 5.5 convolution_convert_fusion.2
  535.8 39.8 %psum.56 = f32[2,1536]{1,0:T(2,128)} all-reduce(f32[2,1536]{1,0:T(2,128)} %pad_maximum_fusion.4), channel_id=1, replica_groups=mesh['fsdp'=4,'ctx'=8] {'fsdp','ctx'}, use_global_device_ids=true, to_apply=%region_23.24 | all-reduce | flops 3072 | bytes 24576 | tf_op jit(solution)/shard_map/psum | solution.py:341
  581.4 392.1 %all-reduce.3.cloned.1.call-done = (bf16[384,1536]{1,0:T(8,128)(2,1)}, bf16[192,1536]{1,0:T(8,128)(2,1)}, bf16[192,1536]{1,0:T(8,128)(2,1)}, bf16[384,1536]{1,0:...) async-done(((bf16[384,1536]{1,0:T(8,128)(2,1)}, bf16[192,1536]{1,0:T(8,128)(2,1)}, bf16[192,1536]{1,0:T(8,128)(2,1)}, ...) | async-done | bytes 12976144 | tf_op jit(solution)/shard_map/psum | solution.py:339
  (356 shorter events, 227.1 us)
Async XLA Ops:
  7.2 232.9 %copy-start = (bf16[1024,1536]{1,0:T(8,128)(2,1)S(1)}, bf16[1024,1536]{1,0:T(8,128)(2,1)}, u32[]{:S(2)}) copy-start(bf16[1024,1536]{1,0:T(8,128)(2,1)} %param.31) | copy-start | bytes 9437188
  7.2 35.2 %all-gather.6.cloned.1.call-start = ((), (), s32[]{:S(2)}) async-start(), calls=%async_computation.6 | async-start | bytes 1966080 | tf_op jit(solution)/shard_map/all_gather | solution.py:205
  7.9 187.2 %reduce-scatter.7.cloned.1.call-start = ((), (), s32[]{:S(2)}) async-start(), calls=%async_computation.7 | async-start | bytes 1966080 | tf_op jit(solution)/shard_map/reduce_scatter | solution.py:209
  8.8 37.7 %copy-start.43 = (f32[1536]{0:T(1024)}, f32[1536]{0:T(1024)S(1)}, u32[]{:S(2)}) copy-start(f32[1536]{0:T(1024)S(1)} %convert_element_type.162) | copy-start | bytes 18436
  15.0 26.9 %copy-start.25 = (s32[4,1,128]{2,1,0:T(1,128)}, s32[4,1,128]{2,1,0:T(1,128)S(1)}, u32[]{:S(2)}) copy-start(s32[4,1,128]{2,1,0:T(1,128)S(1)} %all-gather) | copy-start | bytes 6148
  42.4 18.2 %copy-start.14 = (f32[512,48]{0,1:T(8,128)}, f32[512,48]{0,1:T(8,128)S(1)}, u32[]{:S(2)}) copy-start(f32[512,48]{0,1:T(8,128)S(1)} %get-tuple-element.994) | copy-start | bytes 294916
  42.4 18.2 %copy-start.16 = (f32[512,48]{0,1:T(8,128)}, f32[512,48]{0,1:T(8,128)S(1)}, u32[]{:S(2)}) copy-start(f32[512,48]{0,1:T(8,128)S(1)} %get-tuple-element.995) | copy-start | bytes 294916
  47.4 18.3 %collective-permute-start.7 = (bf16[512,192]{0,1:T(8,128)(2,1)}, bf16[512,192]{0,1:T(8,128)(2,1)}, u32[]{:S(2)}, u32[]{:S(2)}) collective-permute-start(bf16[512,192]{0,1:T(8,128)(2,1)} %bitcast.6), channel_id=1, source_target_pairs={{0,1},{1,2},{2,3},{3,4},{4,5},{5,6},{6,7},{7,0},{8,9},{9,10},{10,1... | collective-permute-start | bytes 589832 | tf_op jit(solution)/shard_map/ppermute | solution.py:23
  48.9 16.8 %collective-permute-start.8 = (bf16[512,192]{0,1:T(8,128)(2,1)}, bf16[512,192]{0,1:T(8,128)(2,1)}, u32[]{:S(2)}, u32[]{:S(2)}) collective-permute-start(bf16[512,192]{0,1:T(8,128)(2,1)} %bitcast.6), channel_id=1, source_target_pairs={{0,7},{1,0},{2,1},{3,2},{4,3},{5,4},{6,5},{7,6},{8,15},{9,8},{10,9... | collective-permute-start | bytes 589832 | tf_op jit(solution)/shard_map/ppermute | solution.py:28
  54.9 15.5 %collective-permute-start = (bf16[512,192]{0,1:T(8,128)(2,1)}, bf16[512,192]{0,1:T(8,128)(2,1)}, u32[]{:S(2)}, u32[]{:S(2)}) collective-permute-start(bf16[512,192]{0,1:T(8,128)(2,1)} %get-tuple-element.997), channel_id=1, source_target_pairs={{0,1},{1,2},{2,3},{3,4},{4,5},{5,6},{6,7},{7,0},{8,9},{9,10},{10,1... | collective-permute-start | bytes 589832 | tf_op jit(solution)/shard_map/ppermute | solution.py:23
  54.9 18.7 %collective-permute-start.1 = (bf16[512,192]{0,1:T(8,128)(2,1)}, bf16[512,192]{0,1:T(8,128)(2,1)}, u32[]{:S(2)}, u32[]{:S(2)}) collective-permute-start(bf16[512,192]{0,1:T(8,128)(2,1)} %get-tuple-element.997), channel_id=1, source_target_pairs={{0,7},{1,0},{2,1},{3,2},{4,3},{5,4},{6,5},{7,6},{8,15},{9,8},{10,9... | collective-permute-start | bytes 589832 | tf_op jit(solution)/shard_map/ppermute | solution.py:28
  65.7 15.9 %collective-permute-start.9 = (bf16[512,192]{0,1:T(8,128)(2,1)}, bf16[512,192]{0,1:T(8,128)(2,1)S(1)}, u32[]{:S(2)}, u32[]{:S(2)}) collective-permute-start(bf16[512,192]{0,1:T(8,128)(2,1)} %collective-permute-done.7), channel_id=1, source_target_pairs={{0,1},{1,2},{2,3},{3,4},{4,5},{5,6},{6,7},{7,0},{8,9},{9,10},{10,1... | collective-permute-start | bytes 589832 | tf_op jit(solution)/shard_map/ppermute | solution.py:23
  65.7 15.9 %collective-permute-start.10 = (bf16[512,192]{0,1:T(8,128)(2,1)}, bf16[512,192]{0,1:T(8,128)(2,1)S(1)}, u32[]{:S(2)}, u32[]{:S(2)}) collective-permute-start(bf16[512,192]{0,1:T(8,128)(2,1)} %collective-permute-done.8), channel_id=1, source_target_pairs={{0,7},{1,0},{2,1},{3,2},{4,3},{5,4},{6,5},{7,6},{8,15},{9,8},{10,9... | collective-permute-start | bytes 589832 | tf_op jit(solution)/shard_map/ppermute | solution.py:28
  70.4 15.9 %collective-permute-start.2 = (bf16[512,192]{0,1:T(8,128)(2,1)}, bf16[512,192]{0,1:T(8,128)(2,1)S(1)}, u32[]{:S(2)}, u32[]{:S(2)}) collective-permute-start(bf16[512,192]{0,1:T(8,128)(2,1)} %collective-permute-done), channel_id=1, source_target_pairs={{0,1},{1,2},{2,3},{3,4},{4,5},{5,6},{6,7},{7,0},{8,9},{9,10},{10,1... | collective-permute-start | bytes 589832 | tf_op jit(solution)/shard_map/ppermute | solution.py:23
  73.7 16.1 %collective-permute-start.3 = (bf16[512,192]{0,1:T(8,128)(2,1)}, bf16[512,192]{0,1:T(8,128)(2,1)S(1)}, u32[]{:S(2)}, u32[]{:S(2)}) collective-permute-start(bf16[512,192]{0,1:T(8,128)(2,1)} %collective-permute-done.1), channel_id=1, source_target_pairs={{0,7},{1,0},{2,1},{3,2},{4,3},{5,4},{6,5},{7,6},{8,15},{9,8},{10,9... | collective-permute-start | bytes 589832 | tf_op jit(solution)/shard_map/ppermute | solution.py:28
  81.6 12.6 %collective-permute-start.11 = (bf16[512,192]{0,1:T(8,128)(2,1)S(1)}, bf16[512,192]{0,1:T(8,128)(2,1)S(1)}, u32[]{:S(2)}, u32[]{:S(2)}) collective-permute-start(bf16[512,192]{0,1:T(8,128)(2,1)S(1)} %collective-permute-done.9), channel_id=1, source_target_pairs={{0,1},{1,2},{2,3},{3,4},{4,5},{5,6},{6,7},{7,0},{8,9},{9,10},{10,1... | collective-permute-start | bytes 589832 | tf_op jit(solution)/shard_map/ppermute | solution.py:23
  81.6 21.3 %collective-permute-start.12 = (bf16[512,192]{0,1:T(8,128)(2,1)S(1)}, bf16[512,192]{0,1:T(8,128)(2,1)S(1)}, u32[]{:S(2)}, u32[]{:S(2)}) collective-permute-start(bf16[512,192]{0,1:T(8,128)(2,1)S(1)} %collective-permute-done.10), channel_id=1, source_target_pairs={{0,7},{1,0},{2,1},{3,2},{4,3},{5,4},{6,5},{7,6},{8,15},{9,8},{10,9... | collective-permute-start | bytes 589832 | tf_op jit(solution)/shard_map/ppermute | solution.py:28
  86.3 12.2 %collective-permute-start.4 = (bf16[512,192]{0,1:T(8,128)(2,1)S(1)}, bf16[512,192]{0,1:T(8,128)(2,1)S(1)}, u32[]{:S(2)}, u32[]{:S(2)}) collective-permute-start(bf16[512,192]{0,1:T(8,128)(2,1)S(1)} %collective-permute-done.2), channel_id=1, source_target_pairs={{0,1},{1,2},{2,3},{3,4},{4,5},{5,6},{6,7},{7,0},{8,9},{9,10},{10,1... | collective-permute-start | bytes 589832 | tf_op jit(solution)/shard_map/ppermute | solution.py:23
  89.8 15.6 %collective-permute-start.5 = (bf16[512,192]{0,1:T(8,128)(2,1)S(1)}, bf16[512,192]{0,1:T(8,128)(2,1)S(1)}, u32[]{:S(2)}, u32[]{:S(2)}) collective-permute-start(bf16[512,192]{0,1:T(8,128)(2,1)S(1)} %collective-permute-done.3), channel_id=1, source_target_pairs={{0,7},{1,0},{2,1},{3,2},{4,3},{5,4},{6,5},{7,6},{8,15},{9,8},{10,9... | collective-permute-start | bytes 589832 | tf_op jit(solution)/shard_map/ppermute | solution.py:28
  94.2 11.8 %collective-permute-start.13 = (bf16[512,192]{0,1:T(8,128)(2,1)S(1)}, bf16[512,192]{0,1:T(8,128)(2,1)S(1)}, u32[]{:S(2)}, u32[]{:S(2)}) collective-permute-start(bf16[512,192]{0,1:T(8,128)(2,1)S(1)} %collective-permute-done.11), channel_id=1, source_target_pairs={{0,1},{1,2},{2,3},{3,4},{4,5},{5,6},{6,7},{7,0},{8,9},{9,10},{10,1... | collective-permute-start | bytes 589832 | tf_op jit(solution)/shard_map/ppermute | solution.py:23
  98.6 9.5 collective-permute-start.6
  168.3 50.7 %all-gather.8.cloned.1.call-start = ((), (), s32[]{:S(2)}) async-start(), calls=%async_computation.8 | async-start | bytes 1966080 | tf_op jit(solution)/shard_map/all_gather | solution.py:205
  199.1 40.9 %all-gather.10.cloned.1.call-start = ((), (), s32[]{:S(2)}) async-start(), calls=%async_computation.10 | async-start | bytes 1966080 | tf_op jit(solution)/shard_map/all_gather | solution.py:205
  199.7 80.4 %reduce-scatter.11.cloned.1.call-start = ((), (), s32[]{:S(2)}) async-start(), calls=%async_computation.11 | async-start | bytes 1966080 | tf_op jit(solution)/shard_map/reduce_scatter | solution.py:209
  252.0 53.2 %all-gather.12.cloned.1.call-start = ((), (), s32[]{:S(2)}) async-start(), calls=%async_computation.12 | async-start | bytes 1966080 | tf_op jit(solution)/shard_map/all_gather | solution.py:205
  285.4 145.7 %reduce-scatter.13.cloned.1.call-start = ((), (), s32[]{:S(2)}) async-start(), calls=%async_computation.13 | async-start | bytes 1769472 | tf_op jit(solution)/shard_map/reduce_scatter | solution.py:269
  364.8 135.2 %reduce-scatter.15.cloned.1.call-start = ((), (), s32[]{:S(2)}) async-start(), calls=%async_computation.14 | async-start | bytes 1769472 | tf_op jit(solution)/shard_map/reduce_scatter | solution.py:269
  374.2 158.3 %reduce-scatter.17.cloned.1.call-start = ((), (), s32[]{:S(2)}) async-start(), calls=%async_computation.15 | async-start | bytes 1966080 | tf_op jit(solution)/shard_map/reduce_scatter | solution.py:209
  504.0 74.2 %reduce-scatter.9.cloned.1.call-start = ((), (), s32[]{:S(2)}) async-start(), calls=%async_computation.9 | async-start | bytes 1966080 | tf_op jit(solution)/shard_map/reduce_scatter | solution.py:209
  508.2 465.2 %all-reduce.3.cloned.1.call-start = ((), (), s32[]{:S(2)}) async-start(), calls=%async_computation.16 | async-start | bytes 25952256 | tf_op jit(solution)/shard_map/psum | solution.py:339
  528.5 49.7 %copy-start.4 = (bf16[128,1536]{1,0:T(8,128)(2,1)S(1)}, bf16[128,1536]{1,0:T(8,128)(2,1)}, u32[]{:S(2)}) copy-start(bf16[128,1536]{1,0:T(8,128)(2,1)} %param.20) | copy-start | bytes 1179652
  528.5 49.7 %copy-start.40 = (f32[1536]{0:T(1024)S(1)}, f32[1536]{0:T(1024)}, u32[]{:S(2)}) copy-start(f32[1536]{0:T(1024)} %convert_element_type.171) | copy-start | bytes 18436
  (79 other events, 261.2 us)
Sparse Core Ops, SparseCore 0:
  9.6 22.3 all-gather.5
  168.4 26.7 reduce-scatter.6
  199.3 19.6 all-gather.7
  220.3 19.6 all-gather.9
  252.1 27.9 reduce-scatter.10
  285.5 19.6 all-gather.11
  365.0 66.0 reduce-scatter.12
  435.1 64.9 reduce-scatter.14
  504.1 26.8 reduce-scatter.16
  533.9 27.9 reduce-scatter.8
  568.8 404.5 all-reduce.2
